TPU v7x, 32 devices: a whole 2x2x4 slice. The times are simulated.
32 devices in a mesh: dp: 2 (over x), tp: 4 (over z), cp: 4 (over y, core).
Axes of the slice: x: 2, y: 2, z: 4, core: 2. Of those that a mesh axis runs over, the one named last changes fastest.
Arguments:
- hidden_in: bfloat16 [512, 4096], P(('dp', 'cp', 'tp')), parts along dimension 0
- positions: int32 [512], P(('dp', 'cp', 'tp')), parts along dimension 0
- cache_len: int32 [2], P('dp'), parts along dimension 0
- cache_k: bfloat16 [65536, 1024], P(('dp', 'cp', 'tp')), parts along dimension 0
- cache_v: bfloat16 [65536, 1024], P(('dp', 'cp', 'tp')), parts along dimension 0
- norm1_gain: bfloat16 [4096], replicated
- w_query: bfloat16 [4096, 4096], P(None, 'tp')
- w_key: bfloat16 [4096, 1024], P(None, 'tp')
- w_value: bfloat16 [4096, 1024], P(None, 'tp')
- w_out: bfloat16 [4096, 4096], P('tp')
- norm2_gain: bfloat16 [4096], replicated
- w_gate: bfloat16 [4096, 12800], P(None, 'tp')
- w_up: bfloat16 [4096, 12800], P(None, 'tp')
- w_down: bfloat16 [12800, 4096], P('tp')
Outputs:
- output: bfloat16 [512, 4096], P(('dp', 'cp', 'tp')), parts along dimension 0
There are 2 independent parts. A program takes and returns all parts, laid end to end along the dimension named above; an argument that names none is the same for every part.
All inputs are finite; a program needn't handle non-finite values.
Results may differ from a plain program's by a relative error of at most 0.011109.
Values are sent between devices in bfloat16 or wider.
A program may use at most 1 GiB of HBM per device.

v0:
```python
import math
import jax
import jax.numpy as jnp
from jax import lax
from jax.sharding import PartitionSpec as P

HEAD_DIM = 128
ROPE_BASE = 500000.0
NORM_EPS = 1e-5


def rms_norm(hidden, norm_gain):
    values = hidden.astype(jnp.float32)
    inv_rms = lax.rsqrt(jnp.mean(values * values, axis=-1, keepdims=True) + NORM_EPS)
    return (values * inv_rms * norm_gain.astype(jnp.float32)).astype(jnp.bfloat16)


def rotary(projected, positions):
    half_dim = HEAD_DIM // 2
    inv_freq = 1.0 / (ROPE_BASE ** (jnp.arange(half_dim, dtype=jnp.float32) * (2.0 / HEAD_DIM)))
    angles = positions.astype(jnp.float32)[:, None] * inv_freq[None, :]
    expand = (angles.shape[0],) + (1,) * (projected.ndim - 2) + (half_dim,)
    cos_table = jnp.cos(angles).reshape(expand)
    sin_table = jnp.sin(angles).reshape(expand)
    first_half = projected[..., :half_dim]
    second_half = projected[..., half_dim:]
    rotated = jnp.concatenate([first_half * cos_table - second_half * sin_table, second_half * cos_table + first_half * sin_table], axis=-1)
    return rotated.astype(jnp.bfloat16)


def attend_rows(block_queries, block_pos, cache_keys, cache_values, cache_valid, new_keys, new_values, all_pos):
    score_scale = 1.0 / math.sqrt(HEAD_DIM)
    cache_scores = jnp.einsum('rkgd,skd->krgs', block_queries, cache_keys, preferred_element_type=jnp.float32) * score_scale
    new_scores = jnp.einsum('rkgd,skd->krgs', block_queries, new_keys, preferred_element_type=jnp.float32) * score_scale
    cache_scores = jnp.where(cache_valid, cache_scores, -jnp.inf)
    causal = all_pos[None, None, None, :] <= block_pos[None, :, None, None]
    new_scores = jnp.where(causal, new_scores, -jnp.inf)
    row_max = jnp.maximum(jnp.max(cache_scores, axis=-1, keepdims=True), jnp.max(new_scores, axis=-1, keepdims=True))
    cache_probs = jnp.exp(cache_scores - row_max)
    new_probs = jnp.exp(new_scores - row_max)
    normalizer = jnp.sum(cache_probs, axis=-1, keepdims=True) + jnp.sum(new_probs, axis=-1, keepdims=True)
    weighted = jnp.einsum('krgs,skd->krgd', cache_probs.astype(jnp.bfloat16), cache_values, preferred_element_type=jnp.float32)
    weighted = weighted + jnp.einsum('krgs,skd->krgd', new_probs.astype(jnp.bfloat16), new_values, preferred_element_type=jnp.float32)
    return jnp.transpose((weighted / normalizer).astype(jnp.bfloat16), (1, 0, 2, 3))


def solution(mesh):
    tp_size = mesh.shape['tp']
    token_spec = P(('dp', 'cp', 'tp'), None)
    column_spec = P(None, 'tp')
    row_spec = P('tp', None)

    def device_layer(hidden_loc, pos_loc, cache_len, cache_k, cache_v, norm1_gain, w_query, w_key, w_value, w_out, norm2_gain, w_gate, w_up, w_down):
        shard_rows = hidden_loc.shape[0]
        kv_local = w_key.shape[1] // HEAD_DIM
        groups = w_query.shape[1] // w_key.shape[1]
        normed = rms_norm(hidden_loc, norm1_gain)
        group_in = lax.all_gather(normed, 'tp', axis=0, tiled=True)
        group_pos = lax.all_gather(pos_loc, 'tp', axis=0, tiled=True)
        group_rows = group_in.shape[0]
        queries = rotary(jnp.dot(group_in, w_query, preferred_element_type=jnp.float32).reshape(group_rows, kv_local, groups, HEAD_DIM), group_pos)
        keys_loc = rotary(jnp.dot(group_in, w_key, preferred_element_type=jnp.float32).reshape(group_rows, kv_local, HEAD_DIM), group_pos)
        values_loc = jnp.dot(group_in, w_value, preferred_element_type=jnp.float32).astype(jnp.bfloat16).reshape(group_rows, kv_local, HEAD_DIM)
        new_keys = lax.all_gather(keys_loc, 'cp', axis=0, tiled=True)
        new_values = lax.all_gather(values_loc, 'cp', axis=0, tiled=True)
        all_pos = lax.all_gather(group_pos, 'cp', axis=0, tiled=True)
        cache_keys = lax.all_gather(lax.all_to_all(cache_k, 'tp', 1, 0, tiled=True), 'cp', axis=0, tiled=True).reshape(-1, kv_local, HEAD_DIM)
        cache_values = lax.all_gather(lax.all_to_all(cache_v, 'tp', 1, 0, tiled=True), 'cp', axis=0, tiled=True).reshape(-1, kv_local, HEAD_DIM)
        cache_valid = jnp.arange(cache_keys.shape[0]) < cache_len[0]
        block_queries = queries.reshape(tp_size, shard_rows, kv_local, groups, HEAD_DIM)
        block_pos = group_pos.reshape(tp_size, shard_rows)

        def attend_block(block_item):
            return attend_rows(block_item[0], block_item[1], cache_keys, cache_values, cache_valid, new_keys, new_values, all_pos)

        attended = lax.map(attend_block, (block_queries, block_pos)).reshape(group_rows, kv_local * groups * HEAD_DIM)
        attn_part = jnp.dot(attended, w_out, preferred_element_type=jnp.float32)
        residual_mid = (hidden_loc.astype(jnp.float32) + lax.psum_scatter(attn_part, 'tp', scatter_dimension=0, tiled=True)).astype(jnp.bfloat16)
        group_mid = lax.all_gather(rms_norm(residual_mid, norm2_gain), 'tp', axis=0, tiled=True)
        gate_proj = jnp.dot(group_mid, w_gate, preferred_element_type=jnp.float32)
        up_proj = jnp.dot(group_mid, w_up, preferred_element_type=jnp.float32)
        hidden_mlp = (jax.nn.silu(gate_proj) * up_proj).astype(jnp.bfloat16)
        mlp_part = jnp.dot(hidden_mlp, w_down, preferred_element_type=jnp.float32)
        return (residual_mid.astype(jnp.float32) + lax.psum_scatter(mlp_part, 'tp', scatter_dimension=0, tiled=True)).astype(jnp.bfloat16)

    return jax.shard_map(device_layer, mesh=mesh, in_specs=(token_spec, P(('dp', 'cp', 'tp')), P('dp'), token_spec, token_spec, P(), column_spec, column_spec, column_spec, row_spec, P(), column_spec, column_spec, row_spec), out_specs=token_spec, check_vma=False)
```

profile of v0, /device:TPU:0, one launch (start us, length us, event | category | flops | bytes accessed | tf_op | source)
XLA Modules:
  0.0 643.0 jit_solution(17458183242209757936)
XLA Ops:
  6.5 6.7 %copy.31 = bf16[2048,1024]{0,1:T(8,128)(2,1)} copy(bf16[2048,1024]{1,0:T(8,128)(2,1)} %param.19) | data formatting | bytes 8388608 | tf_op args[3]
  13.2 100.1 %all_to_all.38 = bf16[2048,4,256]{0,2,1:T(8,128)(2,1)} all-to-all(bf16[2048,4,256]{0,2,1:T(8,128)(2,1)} %bitcast.106), channel_id=1, replica_groups=mesh['dp'=2,'tp'=4,'cp'=4] {'tp'}, dimensions={1} | all-to-all | bytes 8388608 | tf_op jit(solution)/shard_map/all_to_all | solution.py:67
  113.3 6.2 copy.32
  119.6 6.5 %copy.36 = bf16[2048,1024]{0,1:T(8,128)(2,1)} copy(bf16[2048,1024]{1,0:T(8,128)(2,1)} %param.20) | data formatting | bytes 8388608 | tf_op args[4]
  126.1 100.2 %all_to_all.39 = bf16[2048,4,256]{0,2,1:T(8,128)(2,1)} all-to-all(bf16[2048,4,256]{0,2,1:T(8,128)(2,1)} %bitcast.107), channel_id=1, replica_groups=mesh['dp'=2,'tp'=4,'cp'=4] {'tp'}, dimensions={1} | all-to-all | bytes 8388608 | tf_op jit(solution)/shard_map/all_to_all | solution.py:68
  226.3 6.2 copy.37
  232.6 0.6 dynamic-slice
  233.9 0.2 dynamic-update-slice
  234.1 5.6 all-reduce
  239.8 0.1 fusion.37
  240.1 16.6 %all_gather.24 = bf16[64,4096]{1,0:T(8,128)(2,1)S(1)} all-gather(bf16[16,4096]{1,0:T(8,128)(2,1)S(1)} %fusion.39), channel_id=1, replica_groups=mesh['dp'=2,'tp'=4,'cp'=4] {'tp'}, dimensions={0}, use_global_device_ids=true | all-gather | bytes 655360 | tf_op jit(solution)/shard_map/all_gather | solution.py:58
  256.7 0.5 fusion.52
  257.2 4.9 fusion.51
  262.3 0.6 dynamic-slice.1
  262.9 2.0 fusion.30
  265.6 0.2 dynamic-update-slice.1
  265.9 8.7 %all-reduce.1 = s32[256]{0:T(256)S(1)} all-reduce(s32[256]{0:T(256)S(1)} %dynamic-update-slice.1), channel_id=1, replica_groups=mesh['dp'=2,'tp'=4,'cp'=4] {'cp'}, use_global_device_ids=true, to_apply=%add.1 | all-reduce | flops 256 | bytes 2048
  274.6 0.2 multiply_cosine_fusion
  275.1 6.1 all_gather.28
  281.2 6.4 all_gather.30
  287.6 0.2 fusion.49
  288.1 21.2 %copy.33 = bf16[32768,256]{0,1:T(8,128)(2,1)} copy(bf16[32768,256]{1,0:T(8,128)(2,1)} %all-gather.3.cloned.1.call-done) | data formatting | bytes 33554432 | tf_op jit(solution)/shard_map/all_gather | solution.py:67
  309.3 21.2 %copy.41 = bf16[32768,2,128]{2,0,1:T(8,128)(2,1)} copy(bf16[32768,2,128]{0,2,1:T(8,128)(2,1)} %bitcast.100) | data formatting | bytes 33554432
  330.5 13.7 %all-gather.5.cloned.1.call-done = bf16[32768,256]{1,0:T(8,128)(2,1)} async-done(((bf16[8192,256]{1,0:T(8,128)(2,1)}), bf16[32768,256]{1,0:T(8,128)(2,1)}) %all-gather.5.cloned.1.call-update) | async-done | bytes 16777232 | tf_op jit(solution)/shard_map/all_gather | solution.py:68
  344.2 21.2 %copy.38 = bf16[32768,256]{0,1:T(8,128)(2,1)} copy(bf16[32768,256]{1,0:T(8,128)(2,1)} %all-gather.5.cloned.1.call-done) | data formatting | bytes 33554432 | tf_op jit(solution)/shard_map/all_gather | solution.py:68
  365.4 21.2 %copy.42 = bf16[32768,2,128]{2,0,1:T(8,128)(2,1)} copy(bf16[32768,2,128]{0,2,1:T(8,128)(2,1)} %bitcast.101) | data formatting | bytes 33554432
  386.5 139.4 %while.11 = (s32[]{:T(128)}, bf16[4,16,2,4,128]{4,3,2,1,0:T(4,128)(2,1)S(1)}, bf16[4,16,2,4,128]{4,1,0,3,2:T(8,128)(2,1)S(1)}, bf16[32768,2,128]{2,0,1:T(8,128)(...) while((s32[]{:T(128)}, ...), condition=%wide.region_6.7_spmd.clone, body=%wide.region_1.6_spmd.clone.sunk | while | flops 2193936384 | bytes 84919104 | solution.py:76
  386.6 0.3 fusion.85
  386.9 0.7 iota_compare_fusion.2
  387.6 12.7 %fusion.83 = (f32[2,16,4]{1,2,0:T(4,128)S(1)}, f32[2,16,4,32768]{3,1,2,0:T(8,128)}) fusion(bf16[32768,2,128]{2,0,1:T(8,128)(2,1)} %get-tuple-element.231, bf16[4,16,2,4,128]{4,1,0,3,2:T(8,128)(2,1)S(1)} %get-tuple-element.230, s32[]{:T(128)} %get-tuple-element.217, pred[32768]{0:T(1024)(128)(4,1)S(1)} %iota_compare_fusion.2), kind=kOutput, calls=%fused_computation.73.clone.1 | convolution fusion | flops 1086324608 | bytes 33620484 | tf_op jit(solution)/shard_map/while/body/eval_jaxpr/rkgd,skd->krgs/dot_general | solution.py:33
  400.3 0.2 fusion.88
  400.4 8.2 %fusion.87 = f32[2,16,4]{1,2,0:T(4,128)S(1)} fusion(f32[2,16,4,32768]{3,1,2,0:T(8,128)} %get-tuple-element.202, f32[2,16,4]{1,2,0:T(4,128)S(1)} %max.10), kind=kLoop, calls=%fused_computation.7.clone.1 | loop fusion | flops 8388480 | bytes 16778240 | tf_op jit(solution)/shard_map/while/body/eval_jaxpr/reduce_sum | solution.py:41
  408.7 12.4 %fusion.86 = f32[2,16,4,128]{3,1,2,0:T(8,128)S(1)} fusion(bf16[32768,2,128]{2,0,1:T(8,128)(2,1)} %get-tuple-element.235, f32[2,16,4,32768]{3,1,2,0:T(8,128)} %get-tuple-element.202, f32[2,16,4]{1,2,0:T(4,128)S(1)} %max.10), kind=kOutput, calls=%fused_computation.3.clone.1 | convolution fusion | flops 1082130432 | bytes 33620480 | tf_op jit(solution)/shard_map/while/body/eval_jaxpr/krgs,skd->krgd/dot_general | solution.py:42
  421.1 0.2 fusion.89
  421.5 0.3 fusion.85
  421.7 0.7 iota_compare_fusion.2
  422.4 12.7 %fusion.83 = (f32[2,16,4]{1,2,0:T(4,128)S(1)}, f32[2,16,4,32768]{3,1,2,0:T(8,128)}) fusion(bf16[32768,2,128]{2,0,1:T(8,128)(2,1)} %get-tuple-element.231, bf16[4,16,2,4,128]{4,1,0,3,2:T(8,128)(2,1)S(1)} %get-tuple-element.230, s32[]{:T(128)} %get-tuple-element.217, pred[32768]{0:T(1024)(128)(4,1)S(1)} %iota_compare_fusion.2), kind=kOutput, calls=%fused_computation.73.clone.1 | convolution fusion | flops 1086324608 | bytes 33620484 | tf_op jit(solution)/shard_map/while/body/eval_jaxpr/rkgd,skd->krgs/dot_general | solution.py:33
  435.1 0.2 fusion.88
  435.3 8.2 %fusion.87 = f32[2,16,4]{1,2,0:T(4,128)S(1)} fusion(f32[2,16,4,32768]{3,1,2,0:T(8,128)} %get-tuple-element.202, f32[2,16,4]{1,2,0:T(4,128)S(1)} %max.10), kind=kLoop, calls=%fused_computation.7.clone.1 | loop fusion | flops 8388480 | bytes 16778240 | tf_op jit(solution)/shard_map/while/body/eval_jaxpr/reduce_sum | solution.py:41
  443.6 12.4 %fusion.86 = f32[2,16,4,128]{3,1,2,0:T(8,128)S(1)} fusion(bf16[32768,2,128]{2,0,1:T(8,128)(2,1)} %get-tuple-element.235, f32[2,16,4,32768]{3,1,2,0:T(8,128)} %get-tuple-element.202, f32[2,16,4]{1,2,0:T(4,128)S(1)} %max.10), kind=kOutput, calls=%fused_computation.3.clone.1 | convolution fusion | flops 1082130432 | bytes 33620480 | tf_op jit(solution)/shard_map/while/body/eval_jaxpr/krgs,skd->krgd/dot_general | solution.py:42
  456.0 0.2 fusion.89
  456.3 0.3 fusion.85
  456.6 0.7 iota_compare_fusion.2
  457.3 12.7 %fusion.83 = (f32[2,16,4]{1,2,0:T(4,128)S(1)}, f32[2,16,4,32768]{3,1,2,0:T(8,128)}) fusion(bf16[32768,2,128]{2,0,1:T(8,128)(2,1)} %get-tuple-element.231, bf16[4,16,2,4,128]{4,1,0,3,2:T(8,128)(2,1)S(1)} %get-tuple-element.230, s32[]{:T(128)} %get-tuple-element.217, pred[32768]{0:T(1024)(128)(4,1)S(1)} %iota_compare_fusion.2), kind=kOutput, calls=%fused_computation.73.clone.1 | convolution fusion | flops 1086324608 | bytes 33620484 | tf_op jit(solution)/shard_map/while/body/eval_jaxpr/rkgd,skd->krgs/dot_general | solution.py:33
  470.0 0.2 fusion.88
  470.2 8.2 %fusion.87 = f32[2,16,4]{1,2,0:T(4,128)S(1)} fusion(f32[2,16,4,32768]{3,1,2,0:T(8,128)} %get-tuple-element.202, f32[2,16,4]{1,2,0:T(4,128)S(1)} %max.10), kind=kLoop, calls=%fused_computation.7.clone.1 | loop fusion | flops 8388480 | bytes 16778240 | tf_op jit(solution)/shard_map/while/body/eval_jaxpr/reduce_sum | solution.py:41
  478.4 12.4 %fusion.86 = f32[2,16,4,128]{3,1,2,0:T(8,128)S(1)} fusion(bf16[32768,2,128]{2,0,1:T(8,128)(2,1)} %get-tuple-element.235, f32[2,16,4,32768]{3,1,2,0:T(8,128)} %get-tuple-element.202, f32[2,16,4]{1,2,0:T(4,128)S(1)} %max.10), kind=kOutput, calls=%fused_computation.3.clone.1 | convolution fusion | flops 1082130432 | bytes 33620480 | tf_op jit(solution)/shard_map/while/body/eval_jaxpr/krgs,skd->krgd/dot_general | solution.py:42
  490.8 0.2 fusion.89
  491.2 0.3 fusion.85
  491.5 0.7 iota_compare_fusion.2
  492.1 12.7 %fusion.83 = (f32[2,16,4]{1,2,0:T(4,128)S(1)}, f32[2,16,4,32768]{3,1,2,0:T(8,128)}) fusion(bf16[32768,2,128]{2,0,1:T(8,128)(2,1)} %get-tuple-element.231, bf16[4,16,2,4,128]{4,1,0,3,2:T(8,128)(2,1)S(1)} %get-tuple-element.230, s32[]{:T(128)} %get-tuple-element.217, pred[32768]{0:T(1024)(128)(4,1)S(1)} %iota_compare_fusion.2), kind=kOutput, calls=%fused_computation.73.clone.1 | convolution fusion | flops 1086324608 | bytes 33620484 | tf_op jit(solution)/shard_map/while/body/eval_jaxpr/rkgd,skd->krgs/dot_general | solution.py:33
  504.9 0.2 fusion.88
  505.1 8.2 %fusion.87 = f32[2,16,4]{1,2,0:T(4,128)S(1)} fusion(f32[2,16,4,32768]{3,1,2,0:T(8,128)} %get-tuple-element.202, f32[2,16,4]{1,2,0:T(4,128)S(1)} %max.10), kind=kLoop, calls=%fused_computation.7.clone.1 | loop fusion | flops 8388480 | bytes 16778240 | tf_op jit(solution)/shard_map/while/body/eval_jaxpr/reduce_sum | solution.py:41
  513.3 12.4 %fusion.86 = f32[2,16,4,128]{3,1,2,0:T(8,128)S(1)} fusion(bf16[32768,2,128]{2,0,1:T(8,128)(2,1)} %get-tuple-element.235, f32[2,16,4,32768]{3,1,2,0:T(8,128)} %get-tuple-element.202, f32[2,16,4]{1,2,0:T(4,128)S(1)} %max.10), kind=kOutput, calls=%fused_computation.3.clone.1 | convolution fusion | flops 1082130432 | bytes 33620480 | tf_op jit(solution)/shard_map/while/body/eval_jaxpr/krgs,skd->krgd/dot_general | solution.py:42
  525.7 0.2 fusion.89
  526.1 5.9 fusion.53
  532.1 27.4 %reduce-scatter.3.cloned.1.call-done = f32[16,4096]{1,0:T(8,128)} async-done(((f32[64,4096]{1,0:T(8,128)}), f32[16,4096]{1,0:T(8,128)}) %reduce-scatter.3.cloned.1.call-update) | async-done | bytes 262160 | tf_op jit(solution)/shard_map/reduce_scatter | solution.py:78
  559.5 1.1 fusion.41
  560.7 0.5 copy-done.4
  561.3 16.2 %all_gather.31 = bf16[64,4096]{1,0:T(8,128)(2,1)S(1)} all-gather(bf16[16,4096]{1,0:T(8,128)(2,1)S(1)} %fusion.43), channel_id=1, replica_groups=mesh['dp'=2,'tp'=4,'cp'=4] {'tp'}, dimensions={0}, use_global_device_ids=true | all-gather | bytes 655360 | tf_op jit(solution)/shard_map/all_gather | solution.py:79
  577.5 10.8 %fusion.54 = f32[64,3200]{1,0:T(8,128)S(1)} fusion(bf16[64,4096]{1,0:T(8,128)(2,1)S(1)} %all_gather.31, bf16[4096,3200]{1,0:T(8,128)(2,1)} %param.27), kind=kOutput, calls=%fused_computation.80 | convolution fusion | flops 1677721600 | bytes 27557888 | tf_op jit(solution)/shard_map/dot_general | solution.py:80
  588.3 20.7 %fusion.29 = f32[64,4096]{1,0:T(8,128)} fusion(bf16[3200,4096]{1,0:T(8,128)(2,1)} %param.29, bf16[64,4096]{1,0:T(8,128)(2,1)S(1)} %all_gather.31, bf16[4096,3200]{1,0:T(8,128)(2,1)} %param.28, f32[64,3200]{1,0:T(8,128)S(1)} %fusion.54), kind=kOutput, calls=%fused_computation.37 | convolution fusion | flops 3356672000 | bytes 54820864 | tf_op jit(solution)/shard_map/dot_general | solution.py:83
  609.1 25.8 %reduce-scatter.5.cloned.1.call-done = f32[16,4096]{1,0:T(8,128)} async-done(((f32[64,4096]{1,0:T(8,128)}), f32[16,4096]{1,0:T(8,128)}) %reduce-scatter.5.cloned.1.call-update) | async-done | bytes 262160 | tf_op jit(solution)/shard_map/reduce_scatter | solution.py:84
  634.8 1.7 fusion.44
  (69 shorter events, 1.8 us)
Async XLA Ops:
  6.5 250.2 %copy-start = (bf16[4096,256]{1,0:T(8,128)(2,1)S(1)}, bf16[4096,256]{1,0:T(8,128)(2,1)}, u32[]{:S(2)}) copy-start(bf16[4096,256]{1,0:T(8,128)(2,1)} %param.23) | copy-start | bytes 6291460
  6.5 281.6 %all-gather.3.cloned.1.call-start = ((), (), s32[]{:S(2)}) async-start(), calls=%async_computation.4 | async-start | bytes 20971520 | tf_op jit(solution)/shard_map/all_gather | solution.py:67
  119.5 113.1 %copy-start.9 = (u32[32]{0:T(128)S(1)}, u32[32]{0:T(128)}, u32[]{:S(2)}) copy-start(u32[32]{0:T(128)} %constant.43) | copy-start | bytes 388
  119.5 114.3 %copy-start.7 = (s32[16]{0:T(128)S(1)}, s32[16]{0:T(128)}, u32[]{:S(2)}) copy-start(s32[16]{0:T(128)} %param.17) | copy-start | bytes 196
  119.5 120.3 %copy-start.5 = (bf16[4096]{0:T(1024)(128)(2,1)S(1)}, bf16[4096]{0:T(1024)(128)(2,1)}, u32[]{:S(2)}) copy-start(bf16[4096]{0:T(1024)(128)(2,1)} %param.21) | copy-start | bytes 24580
  119.5 120.3 %copy-start.2 = (bf16[16,4096]{1,0:T(8,128)(2,1)S(1)}, bf16[16,4096]{1,0:T(8,128)(2,1)}, u32[]{:S(2)}) copy-start(bf16[16,4096]{1,0:T(8,128)(2,1)} %param.16) | copy-start | bytes 393220
  119.6 224.6 %all-gather.5.cloned.1.call-start = ((), (), s32[]{:S(2)}) async-start(), calls=%async_computation.5 | async-start | bytes 20971520 | tf_op jit(solution)/shard_map/all_gather | solution.py:68
  226.3 36.0 %copy-start.8 = (u32[32]{0:T(128)S(1)}, u32[32]{0:T(128)}, u32[]{:S(2)}) copy-start(u32[32]{0:T(128)} %constant.48) | copy-start | bytes 388
  232.6 327.0 %reduce-scatter.3.cloned.1.call-start = ((), (), s32[]{:S(2)}) async-start(), calls=%async_computation.6 | async-start | bytes 1310720 | tf_op jit(solution)/shard_map/reduce_scatter | solution.py:78
  526.0 6.1 copy-start.6
  526.0 33.5 %copy-start.3 = (bf16[16,4096]{1,0:T(8,128)(2,1)S(1)}, bf16[16,4096]{1,0:T(8,128)(2,1)}, u32[]{:S(2)}) copy-start(bf16[16,4096]{1,0:T(8,128)(2,1)} %param.16) | copy-start | bytes 393220
  532.1 102.8 %reduce-scatter.5.cloned.1.call-start = ((), (), s32[]{:S(2)}) async-start(), calls=%async_computation.7 | async-start | bytes 1310720 | tf_op jit(solution)/shard_map/reduce_scatter | solution.py:84
  560.6 0.7 copy-start.4
  588.3 48.2 %copy-start.1 = (bf16[4096,256]{1,0:T(8,128)(2,1)S(1)}, bf16[4096,256]{1,0:T(8,128)(2,1)}, u32[]{:S(2)}) copy-start(bf16[4096,256]{1,0:T(8,128)(2,1)} %param.23) | copy-start | bytes 6291460
Sparse Core Ops, SparseCore 0:
  119.7 110.2 all-gather.2
  232.7 111.4 all-gather.4
  532.2 27.2 reduce-scatter.2
  609.2 25.5 reduce-scatter.4
where the time goes:
time: 646 us; the launch traced here: 643 us
  blocking collectives  260 us (40%)
  matrix products  147 us (23%)
  local copies, waits for them, and re-layouts  113 us (17%)
  waiting for transfers between devices  67 us (10%)
  other arithmetic  40.3 us (6%)
  between operations  14.6 us (2%)
    all_to_all x1, blocking collectives, device_layer(): lax.all_to_all(cache_v, 'tp', 1, 0, tiled=True)  100 us
    all_to_all x1, blocking collectives, device_layer(): lax.all_to_all(cache_k, 'tp', 1, 0, tiled=True)  100 us
    unnamed x30, local copies, waits for them, and re-layouts  57.8 us
    dot_general x4, matrix products, attend_rows(): jnp.einsum('rkgd,skd->krgs', block_queries, cache_keys, preferred_element...  50.9 us
    dot_general x4, matrix products, attend_rows(): jnp.einsum('krgs,skd->krgd', cache_probs.astype(jnp.bfloat16), cache_valu...  49.7 us
    reduce_sum x4, other arithmetic, attend_rows(): jnp.sum(cache_probs, axis=-1, keepdims=True)  32.9 us
    reduce_scatter x1, waiting for transfers between devices, device_layer(): lax.psum_scatter(attn_part, 'tp', scatter_dimension=0, tiled=True)  27.4 us
    reduce_scatter x1, waiting for transfers between devices, device_layer(): lax.psum_scatter(mlp_part, 'tp', scatter_dimension=0, tiled=True)  25.8 us
  transfers between devices with their start and end apart: 4, of which 3 were waited for; matrix products, arithmetic and copies ran while one was open for 10% of the time, Pallas kernels for 0%

commit v1 on v0

v1 whole, which is shorter than its diff:
```python
import functools
import math
import jax
import jax.numpy as jnp
from jax import lax
from jax.experimental import pallas as pl
from jax.experimental.pallas import tpu as pltpu
from jax.sharding import PartitionSpec as P

HEAD_DIM = 128
ROPE_BASE = 500000.0
NORM_EPS = 1e-5
MESH = pl.DeviceIdType.MESH
TP = 4
CP = 4
EXP_SCALE = math.log2(math.e) / math.sqrt(HEAD_DIM)
LOW = -3.0e38
BF = jnp.bfloat16
F32 = jnp.float32


def dev(t, c):
    return {"tp": t, "cp": c}


def entry_barrier(peers):
    barrier = pltpu.get_barrier_semaphore()
    for t, c in peers:
        pl.semaphore_signal(barrier, inc=1, device_id=dev(t, c), device_id_type=MESH)
    pl.semaphore_wait(barrier, len(peers))


def rcopy(src, dst, send, recv, t, c):
    return pltpu.make_async_remote_copy(src_ref=src, dst_ref=dst, send_sem=send, recv_sem=recv,
                                        device_id=dev(t, c), device_id_type=MESH)


def norm_rows(values, gain):
    values = values.astype(F32)
    inv_rms = lax.rsqrt(jnp.mean(values * values, axis=-1, keepdims=True) + NORM_EPS)
    return (values * inv_rms * gain.astype(F32)).astype(BF)


def qkv_kernel(rows, x_ref, g_ref, cos_ref, sin_ref, wq_hbm, wk_hbm, wv_hbm, qg_ref, k_ref, v_ref,
               wq, wk, wv, xg, act, wsem, xsend, xrecv, qsend, qrecv):
    t = lax.axis_index("tp")
    c = lax.axis_index("cp")
    group_rows = rows * TP
    wcopies = []
    for i, (src, dst) in enumerate(((wq_hbm, wq), (wk_hbm, wk), (wv_hbm, wv))):
        cp = pltpu.make_async_copy(src, dst, wsem.at[i])
        cp.start()
        wcopies.append(cp)
    zpeers = [lax.rem(t + d, TP) for d in (1, 3, 2)]
    cy = lax.rem(c + 2, CP)
    cc = c + 1 - 2 * lax.rem(c, 2)
    entry_barrier([(z, c) for z in zpeers] + [(t, cy), (t, cc)])
    sends = []
    for i, z in enumerate(zpeers):
        cp = rcopy(x_ref, xg.at[t], xsend.at[i], xrecv.at[t], z, c)
        cp.start()
        sends.append(cp)
    act[pl.ds(pl.multiple_of(t * rows, rows), rows), :] = norm_rows(x_ref[...], g_ref[...])
    for i, z in enumerate(zpeers):
        rcopy(x_ref, xg.at[z], xsend.at[i], xrecv.at[z], z, c).wait_recv()
        act[pl.ds(pl.multiple_of(z * rows, rows), rows), :] = norm_rows(xg[z], g_ref[...])
    cos = cos_ref[...]
    sin = sin_ref[...]

    def rotate(part):
        return (part * cos + pltpu.roll(part, HEAD_DIM // 2, 1) * sin).astype(BF)

    wcopies[0].wait()
    a = act[...]
    groups = wq.shape[1] // wk.shape[1]
    kv_local = wk.shape[1] // HEAD_DIM
    for kv in range(kv_local):
        width = groups * HEAD_DIM
        qh = jnp.dot(a, wq[:, kv * width:(kv + 1) * width], preferred_element_type=F32)
        for g in range(groups):
            qg_ref[c, t, kv, g * group_rows:(g + 1) * group_rows, :] = rotate(qh[:, g * HEAD_DIM:(g + 1) * HEAD_DIM])
    own = qg_ref.at[c, t]
    started = []

    def push(block, n, cb, tb, tz, cz):
        cp = rcopy(block, block, qsend.at[n], qrecv.at[cb, tb], tz, cz)
        cp.start()
        started.append(cp)

    def arrive(cb, tb):
        blk = qg_ref.at[cb, tb]
        rcopy(blk, blk, qsend.at[0], qrecv.at[cb, tb], t, cy).wait_recv()
        return blk

    n = 0
    for z in zpeers:
        push(own, n, c, t, z, c)
        n += 1
    push(own, n, c, t, t, cy)
    push(own, n + 1, c, t, t, cc)
    n += 2
    wcopies[1].wait()
    wcopies[2].wait()
    kn = jnp.dot(a, wk[...], preferred_element_type=F32)
    vn = jnp.dot(a, wv[...], preferred_element_type=F32)
    for kv in range(kv_local):
        sl = slice(kv * HEAD_DIM, (kv + 1) * HEAD_DIM)
        k_ref[:, sl] = rotate(kn[:, sl])
    v_ref[...] = vn.astype(BF)
    blk = arrive(cy, t)
    push(blk, n, cy, t, t, cc)
    n += 1
    for z in zpeers:
        blk = arrive(c, z)
        push(blk, n, c, z, t, cy)
        push(blk, n + 1, c, z, t, cc)
        n += 2
    for z in zpeers:
        blk = arrive(cy, z)
        push(blk, n, cy, z, t, cc)
        n += 1
    cd = lax.rem(cc + 2, CP)
    for z in [t] + zpeers:
        arrive(cc, z)
        arrive(cd, z)
    for cp in sends + started:
        cp.wait_send()


def merge(a_ref, b):
    a = a_ref[...]
    ma, mb = a[128:129], b[128:129]
    top = jnp.maximum(ma, mb)
    wa = jnp.exp2((ma - top) * EXP_SCALE)
    wb = jnp.exp2((mb - top) * EXP_SCALE)
    o = a[:128] * wa + b[:128] * wb
    ell = a[129:130] * wa + b[129:130] * wb
    return o, top, ell


def put(ref, o, m, ell):
    ref[0:128, :] = o
    ref[128:136, :] = jnp.concatenate([m, ell, jnp.zeros((6, m.shape[1]), F32)], axis=0)


def attn_kernel(slots, rows, len_ref, q_ref, k_hbm, v_hbm, kn_ref, vn_ref, att_ref,
                kbuf, vbuf, vt, bias, nbias, probs, dsend, drecv, ysend, yrecv, zsend, zrecv, keep,
                ksem, dss, drs, yss, yrs, zss, zrs):
    t = lax.axis_index("tp")
    c = lax.axis_index("cp")
    core = lax.rem(c, 2)
    yi = c // 2
    cy = lax.rem(c + 2, CP)
    cc = c + 1 - 2 * core
    nkv = k_hbm.shape[1] // HEAD_DIM
    per_t = nkv // TP
    group_rows = rows * TP
    nq = q_ref.shape[3]

    def head_of(step):
        return lax.rem(t + 1 + step // per_t, TP) * per_t + lax.rem(step, per_t)

    def kv_copies(step):
        h = head_of(step)
        col = pl.ds(pl.multiple_of(h * HEAD_DIM, HEAD_DIM), HEAD_DIM)
        return (pltpu.make_async_copy(k_hbm.at[:, col], kbuf.at[step], ksem.at[step, 0]),
                pltpu.make_async_copy(v_hbm.at[:, col], vbuf.at[step], ksem.at[step, 1]))

    for s in range(nkv):
        for cp in kv_copies(s):
            cp.start()
    zpeers = [lax.rem(t + d, TP) for d in (1, 2, 3)]
    entry_barrier([(z, c) for z in zpeers] + [(t, cy), (t, cc)])
    base = (c * TP + t) * slots
    slot = base + lax.broadcasted_iota(jnp.int32, (slots, HEAD_DIM), 0)
    bias[...] = jnp.where(slot < len_ref[0], 0.0, -jnp.inf).astype(F32)

    def rel(device, w):
        half = rows // 2
        seg = jnp.where(w < half, device, 2 * TP * CP - 1 - device)
        return seg * half + lax.rem(w, half)

    ki = lax.broadcasted_iota(jnp.int32, (group_rows, nq), 0)
    qi = lax.rem(lax.broadcasted_iota(jnp.int32, (group_rows, nq), 1), group_rows)
    krel = rel(c * TP + ki // rows, lax.rem(ki, rows))
    for cq in range(CP):
        qrel = rel(cq * TP + qi // rows, lax.rem(qi, rows))
        nbias[cq] = jnp.where(krel <= qrel, 0.0, -jnp.inf).astype(F32)

    def tile(step, h, cq, local):
        tq = h // per_t
        q = q_ref[cq, tq, lax.rem(h, per_t)]
        dims = (((1,), (1,)), ((), ()))
        s = lax.dot_general(kbuf[step], q, dims, preferred_element_type=F32)
        b = bias[...]
        s = s + jnp.concatenate([b] * (nq // HEAD_DIM), axis=1)
        m = jnp.maximum(jnp.max(s, axis=0, keepdims=True), LOW)
        if local is not None:
            s2 = lax.dot_general(kn_ref[:, local * HEAD_DIM:(local + 1) * HEAD_DIM], q, dims, preferred_element_type=F32)
            s2 = s2 + nbias[cq]
            m = jnp.maximum(m, jnp.max(s2, axis=0, keepdims=True))
        e = jnp.exp2((s - m) * EXP_SCALE)
        ell = jnp.sum(e, axis=0, keepdims=True)
        o = jnp.dot(vt[...], e.astype(BF), preferred_element_type=F32)
        if local is not None:
            e2 = jnp.exp2((s2 - m) * EXP_SCALE)
            ell = ell + jnp.sum(e2, axis=0, keepdims=True)
            o = o + lax.dot_general(vn_ref[:, local * HEAD_DIM:(local + 1) * HEAD_DIM], e2.astype(BF),
                                    (((0,), (0,)), ((), ())), preferred_element_type=F32)
        return o, m, ell

    def d_copy(step, j):
        return rcopy(dsend.at[step, j], drecv.at[step, j], dss.at[step, j], drs.at[step, j], t, cc)

    def y_copy(step):
        return rcopy(ysend.at[step], yrecv.at[step], yss.at[step], yrs.at[step], t, cy)

    def z_copy(step, h):
        owner = h // per_t
        return rcopy(zsend.at[step], zrecv.at[step], zss.at[step], zrs.at[step], owner, c)

    def head(step, local):
        h = head_of(step)
        for cp in kv_copies(step):
            cp.wait()
        vt[...] = vbuf[step].T
        for j in range(2):
            put(dsend.at[step, j], *tile(step, h, j * 2 + 1 - core, local))
            d_copy(step, j).start()
        put(ysend.at[step], *tile(step, h, (1 - yi) * 2 + core, local))
        put(keep.at[step], *tile(step, h, yi * 2 + core, local))
        d_copy(step, 1 - yi).wait_recv()
        put(ysend.at[step], *merge(ysend.at[step], drecv[step, 1 - yi]))
        y_copy(step).start()
        d_copy(step, yi).wait_recv()
        put(keep.at[step], *merge(keep.at[step], drecv[step, yi]))

    def finish_y(step):
        y_copy(step).wait_recv()
        put(zsend.at[step], *merge(keep.at[step], yrecv[step]))

    far = nkv - per_t

    def loop(step, carry):
        head(step, None)

        @pl.when(step > 0)
        def _():
            finish_y(step - 1)
            z_copy(step - 1, head_of(step - 1)).start()
        return carry

    lax.fori_loop(0, far, loop, 0)
    for i in range(per_t):
        head(far + i, i)
        finish_y(far + i - 1)
        if i == 0:
            z_copy(far - 1, head_of(far - 1)).start()
    finish_y(nkv - 1)
    for i in range(per_t):
        own = zsend.at[far + i]
        for d in range(TP - 1):
            step = d * per_t + i
            rcopy(zsend.at[step], zrecv.at[step], zss.at[step], zrs.at[step], zpeers[d], c).wait_recv()
            o, m, ell = merge(own, zrecv[step])
            put(own, o, m, ell)
        out = (own[0:128, :] / own[129:130, :]).T.astype(BF)
        groups = nq // group_rows
        for g in range(groups):
            hd = i * groups + g
            att_ref[:, hd * HEAD_DIM:(hd + 1) * HEAD_DIM] = out[g * group_rows:(g + 1) * group_rows, :]

    def drain(step, carry):
        for j in range(2):
            d_copy(step, j).wait_send()
        y_copy(step).wait_send()

        @pl.when(step < far)
        def _():
            z_copy(step, head_of(step)).wait_send()
        return carry

    lax.fori_loop(0, nkv, drain, 0)


def mlp_kernel(rows, gchunk, dchunk, ochunk, att_ref, x_ref, g_ref, wo_hbm, wg_hbm, wu_hbm, wd_hbm, out_ref,
               wo, wg, wu, wd, part, rs1, rs2, hid, hg, act, ubuf, wosem, gsem, dsem,
               rss, rrs, hss, hrs, r2s, r2r):
    t = lax.axis_index("tp")
    c = lax.axis_index("cp")
    width = wo_hbm.shape[1]
    ffn = wg_hbm.shape[1]
    n_o = width // ochunk
    n_g = ffn // gchunk
    n_d = width // dchunk
    gslots = wg.shape[0]
    dslots = wd.shape[0]

    def o_copy(j):
        return pltpu.make_async_copy(wo_hbm.at[:, j * ochunk:(j + 1) * ochunk], wo.at[:, j * ochunk:(j + 1) * ochunk], wosem.at[j])

    def g_copy(j):
        cols = slice(j * gchunk, (j + 1) * gchunk)
        return (pltpu.make_async_copy(wg_hbm.at[:, cols], wg.at[j % gslots], gsem.at[j, 0]),
                pltpu.make_async_copy(wu_hbm.at[:, cols], wu.at[j % gslots], gsem.at[j, 1]))

    def d_copy(j):
        return pltpu.make_async_copy(wd_hbm.at[:, j * dchunk:(j + 1) * dchunk], wd.at[j % dslots], dsem.at[j])

    for j in range(n_o):
        o_copy(j).start()
    for j in range(min(gslots, n_g)):
        for cp in g_copy(j):
            cp.start()
    for j in range(min(dslots, n_d)):
        d_copy(j).start()
    zpeers = [lax.rem(t + d, TP) for d in (2, 1, 3)]
    entry_barrier([(z, c) for z in zpeers])
    sends = []

    def row_ds(z):
        return pl.ds(pl.multiple_of(z * rows, rows), rows)

    a = att_ref[...]
    for j in range(n_o):
        cols = slice(j * ochunk, (j + 1) * ochunk)
        o_copy(j).wait()
        part[:, cols] = jnp.dot(a, wo[:, cols], preferred_element_type=F32)
        for i, z in enumerate(zpeers):
            cp = rcopy(part.at[row_ds(z), cols], rs1.at[t, :, cols], rss.at[i, j], rrs.at[t, j], z, c)
            cp.start()
            sends.append(cp)
    for j in range(n_o):
        cols = slice(j * ochunk, (j + 1) * ochunk)
        total = part[row_ds(t), cols]
        for i, z in enumerate(zpeers):
            rcopy(part.at[row_ds(z), cols], rs1.at[z, :, cols], rss.at[i, j], rrs.at[z, j], z, c).wait_recv()
            total = total + rs1[z, :, cols]
        hid[:, cols] = (x_ref[:, cols].astype(F32) + total).astype(BF)
        for i, z in enumerate(zpeers):
            cp = rcopy(hid.at[:, cols], hg.at[t, :, cols], hss.at[i, j], hrs.at[t, j], z, c)
            cp.start()
            sends.append(cp)
    act[row_ds(t), :] = norm_rows(hid[...], g_ref[...])
    for i, z in enumerate(zpeers):
        for j in range(n_o):
            cols = slice(j * ochunk, (j + 1) * ochunk)
            rcopy(hid.at[:, cols], hg.at[z, :, cols], hss.at[i, j], hrs.at[z, j], z, c).wait_recv()
        act[row_ds(z), :] = norm_rows(hg[z], g_ref[...])
    for cp in sends:
        cp.wait_send()
    b = act[...]
    for j in range(n_g):
        for cp in g_copy(j):
            cp.wait()
        gate = jnp.dot(b, wg[j % gslots], preferred_element_type=F32)
        up = jnp.dot(b, wu[j % gslots], preferred_element_type=F32)
        ubuf[:, j * gchunk:(j + 1) * gchunk] = (jax.nn.silu(gate) * up).astype(BF)
        if j + gslots < n_g:
            for cp in g_copy(j + gslots):
                cp.start()
    u = ubuf[...]
    sends = []
    for j in range(n_d):
        cols = slice(j * dchunk, (j + 1) * dchunk)
        d_copy(j).wait()
        part[:, cols] = jnp.dot(u, wd[j % dslots], preferred_element_type=F32)
        if j + dslots < n_d:
            d_copy(j + dslots).start()
        for i, z in enumerate(zpeers):
            cp = rcopy(part.at[row_ds(z), cols], rs2.at[t, :, cols], r2s.at[i, j], r2r.at[t, j], z, c)
            cp.start()
            sends.append(cp)
    for j in range(n_d):
        cols = slice(j * dchunk, (j + 1) * dchunk)
        total = part[row_ds(t), cols]
        for i, z in enumerate(zpeers):
            rcopy(part.at[row_ds(z), cols], rs2.at[z, :, cols], r2s.at[i, j], r2r.at[z, j], z, c).wait_recv()
            total = total + rs2[z, :, cols]
        out_ref[:, cols] = (hid[:, cols].astype(F32) + total).astype(BF)
    for cp in sends:
        cp.wait_send()


VM = pl.BlockSpec(memory_space=pltpu.VMEM)
SM = pl.BlockSpec(memory_space=pltpu.SMEM)
ANY = pl.BlockSpec(memory_space=pl.ANY)
DMA = pltpu.SemaphoreType.DMA


def params(cid, mib):
    return pltpu.CompilerParams(collective_id=cid, has_side_effects=True, vmem_limit_bytes=mib * 1024 * 1024)


def solution(mesh):
    token_spec = P(('dp', 'cp', 'tp'), None)
    column_spec = P(None, 'tp')
    row_spec = P('tp', None)

    def device_layer(x, pos, cache_len, cache_k, cache_v, gain1, wq, wk, wv, wo, gain2, wg, wu, wd):
        rows, width = x.shape
        group_rows = rows * TP
        kv_local = wk.shape[1] // HEAD_DIM
        groups = wq.shape[1] // wk.shape[1]
        nq = groups * group_rows
        c = lax.axis_index("cp")
        half = rows // 2
        idx = jnp.arange(group_rows, dtype=jnp.int32)
        device = c * TP + idx // rows
        within = idx % rows
        seg = jnp.where(within < half, device, 2 * TP * CP - 1 - device)
        group_pos = cache_len[0] + seg * half + within % half
        half_dim = HEAD_DIM // 2
        inv_freq = 1.0 / (ROPE_BASE ** (jnp.arange(half_dim, dtype=F32) * (2.0 / HEAD_DIM)))
        angles = group_pos.astype(F32)[:, None] * inv_freq[None, :]
        cos, sin = jnp.cos(angles), jnp.sin(angles)
        cos2 = jnp.concatenate([cos, cos], axis=1)
        sin2 = jnp.concatenate([-sin, sin], axis=1)
        qg, kn, vn = pl.pallas_call(
            functools.partial(qkv_kernel, rows),
            out_shape=(jax.ShapeDtypeStruct((CP, TP, kv_local, nq, HEAD_DIM), BF),
                       jax.ShapeDtypeStruct((group_rows, wk.shape[1]), BF),
                       jax.ShapeDtypeStruct((group_rows, wk.shape[1]), BF)),
            in_specs=[VM, VM, VM, VM, ANY, ANY, ANY],
            out_specs=(VM, VM, VM),
            scratch_shapes=[pltpu.VMEM(wq.shape, BF), pltpu.VMEM(wk.shape, BF), pltpu.VMEM(wv.shape, BF),
                            pltpu.VMEM((TP, rows, width), BF), pltpu.VMEM((group_rows, width), BF),
                            DMA((3,)), DMA((3,)), DMA((TP,)), DMA((15,)), DMA((CP, TP))],
            compiler_params=params(0, 40), name="qkv",
        )(x, gain1.reshape(1, width), cos2, sin2, wq, wk, wv)
        slots = cache_k.shape[0]
        nkv = cache_k.shape[1] // HEAD_DIM
        att = pl.pallas_call(
            functools.partial(attn_kernel, slots, rows),
            out_shape=jax.ShapeDtypeStruct((group_rows, wq.shape[1]), BF),
            in_specs=[SM, VM, ANY, ANY, VM, VM],
            out_specs=VM,
            scratch_shapes=[pltpu.VMEM((nkv, slots, HEAD_DIM), BF), pltpu.VMEM((nkv, slots, HEAD_DIM), BF),
                            pltpu.VMEM((HEAD_DIM, slots), BF), pltpu.VMEM((slots, HEAD_DIM), F32),
                            pltpu.VMEM((CP, group_rows, nq), F32), pltpu.VMEM((8, 128), BF),
                            pltpu.VMEM((nkv, 2, 136, nq), F32), pltpu.VMEM((nkv, 2, 136, nq), F32),
                            pltpu.VMEM((nkv, 136, nq), F32), pltpu.VMEM((nkv, 136, nq), F32),
                            pltpu.VMEM((nkv, 136, nq), F32), pltpu.VMEM((nkv, 136, nq), F32),
                            pltpu.VMEM((nkv, 136, nq), F32),
                            DMA((nkv, 2)), DMA((nkv, 2)), DMA((nkv, 2)), DMA((nkv,)), DMA((nkv,)),
                            DMA((nkv,)), DMA((nkv,))],
            compiler_params=params(1, 60), name="attn",
        )(cache_len, qg, cache_k, cache_v, kn, vn)
        ffn = wg.shape[1]
        gchunk, dchunk, ochunk = ffn // 5, width // 8, width // 4
        n_o, n_g, n_d = 4, 5, 8
        out = pl.pallas_call(
            functools.partial(mlp_kernel, rows, gchunk, dchunk, ochunk),
            out_shape=jax.ShapeDtypeStruct((rows, width), BF),
            in_specs=[VM, VM, VM, ANY, ANY, ANY, ANY],
            out_specs=VM,
            scratch_shapes=[pltpu.VMEM(wo.shape, BF), pltpu.VMEM((3, width, gchunk), BF), pltpu.VMEM((3, width, gchunk), BF),
                            pltpu.VMEM((3, ffn, dchunk), BF), pltpu.VMEM((group_rows, width), F32),
                            pltpu.VMEM((TP, rows, width), F32), pltpu.VMEM((TP, rows, width), F32),
                            pltpu.VMEM((rows, width), BF), pltpu.VMEM((TP, rows, width), BF),
                            pltpu.VMEM((group_rows, width), BF), pltpu.VMEM((group_rows, ffn), BF),
                            DMA((n_o,)), DMA((n_g, 2)), DMA((n_d,)),
                            DMA((3, n_o)), DMA((TP, n_o)), DMA((3, n_o)), DMA((TP, n_o)), DMA((3, n_d)), DMA((TP, n_d))],
            compiler_params=params(2, 62), name="mlp",
        )(att, x, gain2.reshape(1, width), wo, wg, wu, wd)
        return out

    return jax.shard_map(device_layer, mesh=mesh, in_specs=(token_spec, P(('dp', 'cp', 'tp')), P('dp'), token_spec, token_spec, P(), column_spec, column_spec, column_spec, row_spec, P(), column_spec, column_spec, row_spec), out_specs=token_spec, check_vma=False)
```

time: 646 us -> 182 us (0.28)
  blocking collectives: 260 us -> 0 us
  Pallas kernels: 0 us -> 171 us
  matrix products: 147 us -> 0 us
  local copies, waits for them, and re-layouts: 113 us -> 9.53 us
  waiting for transfers between devices: 67 us -> 0 us
  other arithmetic: 40.3 us -> 0.3 us
  between operations: 14.6 us -> 0.74 us
    all_to_all x2 -> x0, blocking collectives: 200 us -> none  [the longest x1 100 us: device_layer(): lax.all_to_all(cache_v, 'tp', 1, 0, tiled=True)]
    pallas_call x0 -> x3, Pallas kernels: none -> 171 us  [the longest x1 77.7 us: device_layer(): pl.pallas_call(functools.partial(mlp_kernel, rows, gchunk, dchunk, ochunk...]
    dot_general x22 -> x0, matrix products: 147 us -> none  [the longest x4 50.9 us: attend_rows(): jnp.einsum('rkgd,skd->krgs', block_queries, cache_keys, preferred_element...]
    reduce_scatter x2 -> x0, waiting for transfers between devices: 53.2 us -> none  [the longest x1 27.4 us: device_layer(): lax.psum_scatter(attn_part, 'tp', scatter_dimension=0, tiled=True)]
    unnamed x30 -> x15, local copies, waits for them, and re-layouts: 57.8 us -> 8.21 us
    all_gather x4 -> x0, blocking collectives: 45.4 us -> none  [the longest x1 16.6 us: device_layer(): group_in = lax.all_gather(normed, 'tp', axis=0, tiled=True)]
    all_gather x2 -> x0, local copies, waits for them, and re-layouts: 42.4 us -> none  [the longest x1 21.2 us: device_layer(): lax.all_gather(lax.all_to_all(cache_k, 'tp', 1, 0, tiled=True), 'cp', axi...]
    reduce_sum x10 -> x0, other arithmetic: 34.8 us -> none  [the longest x4 32.9 us: attend_rows(): jnp.sum(cache_probs, axis=-1, keepdims=True)]
  transfers between devices with their start and end apart: 4 -> 0, of which waited for: 3 -> 0; matrix products, arithmetic and copies ran while one was open for 10% -> 0% of each run, Pallas kernels for 0% -> 0%
where the time goes in v1:
time: 182 us; the launch traced here: 181 us
  Pallas kernels  171 us (94%)
  local copies, waits for them, and re-layouts  9.53 us (5%)
    pallas_call x1, Pallas kernels, device_layer(): pl.pallas_call(functools.partial(mlp_kernel, rows, gchunk, dchunk, ochunk...  77.7 us
    pallas_call x1, Pallas kernels, device_layer(): pl.pallas_call(functools.partial(attn_kernel, slots, rows), out_shape=jax...  58.6 us
    pallas_call x1, Pallas kernels, device_layer(): pl.pallas_call(functools.partial(qkv_kernel, rows), out_shape=(jax.ShapeD...  34.4 us
    unnamed x15, local copies, waits for them, and re-layouts  8.21 us

profile of v1, /device:TPU:0, one launch (start us, length us, event | category | flops | bytes accessed | tf_op | source)
XLA Modules:
  0.0 181.4 jit_solution(13713197170223239659)
XLA Ops:
  0.7 0.2 fusion
  0.9 0.1 pad_maximum_fusion
  1.0 0.7 reshape.51.g_ref
  1.7 0.0 copy-start
  1.7 1.6 copy-done
  3.3 0.0 copy-start.1
  3.3 1.6 copy-done.1
  4.9 0.0 copy-start.3
  4.9 0.9 copy-done.3
  5.8 34.4 %qkv.1 = (bf16[4,4,2,256,128]{4,3,2,1,0:T(8,128)(2,1)S(1)}, bf16[64,256]{1,0:T(8,128)(2,1)S(1)}, bf16[64,256]{1,0:T(8,128)(2,1)S(1)}) custom-call(bf16[16,4096]{1,0:T(8,128)(2,1)S(1)} %copy-done.3, bf16[1,4096]{1,0:T(2,128)(2,1)S(1)} %reshape.51.g_ref, f32[64,128]{1,0:T(8,128)S(1)} %get-tuple-element.14.cos_ref, f32[64,128]{1,0:T(8,128)S(1)} %get-tuple-element.15.sin_ref, ...), custom_call_target="tpu_custom_call" | custom-call | tf_op jit(solution)/shard_map/qkv/pallas_call | solution.py:419
  40.2 0.0 copy-start.2
  40.2 1.3 copy-done.2
  41.6 0.0 copy-start.4
  41.6 0.6 copy-done.4
  42.2 0.0 copy-start.5
  42.2 0.6 copy-done.5
  42.8 0.0 copy-start.6
  42.8 58.6 %attn.1.att_ref = bf16[64,1024]{1,0:T(8,128)(2,1)} custom-call(s32[1]{0:T(128)} %copy.15.len_ref, bf16[4,4,2,256,128]{4,3,2,1,0:T(8,128)(2,1)} %copy-done.2, bf16[2048,1024]{1,0:T(8,128)(2,1)} %k_hbm.1, bf16[2048,1024]{1,0:T(8,128)(2,1)} %v_hbm.1, bf16[64,256]{1,0:T(8,128)(2,1)} %copy-done.4, bf16[64,256]{1,0:T(8,128)(2,1)} %copy-done.5), custom_call_target="tpu_custom_call" | custom-call | tf_op jit(solution)/shard_map/attn/pallas_call | solution.py:433
  101.4 0.0 copy-done.6
  101.5 0.6 reshape.52.g_ref
  102.1 77.7 %mlp.1 = bf16[16,4096]{1,0:T(8,128)(2,1)} custom-call(bf16[64,1024]{1,0:T(8,128)(2,1)} %attn.1.att_ref, bf16[16,4096]{1,0:T(8,128)(2,1)} %x_ref.3, bf16[1,4096]{1,0:T(2,128)(2,1)} %reshape.52.g_ref, bf16[1024,4096]{1,0:T(8,128)(2,1)} %wo_hbm.1, bf16[4096,3200]{1,0:T(8,128)(2,1)} %wg_hbm.1, bf16[4096,3200]{1,0:T(8,128)(2,1)} %wu_hbm.1, bf16[3200,4096]{1,0:T(8,128)(2,1)} %wd_hbm.1), custom_call_target="tpu_custom_call" | custom-call | tf_op jit(solution)/shard_map/mlp/pallas_call | solution.py:452
  179.8 1.6 copy.16
  (2 shorter events, 0.0 us)
Async XLA Ops:
  1.7 1.6 copy-start
  3.3 1.6 copy-start.1
  4.9 0.9 copy-start.3
  40.2 1.3 copy-start.2
  41.6 0.6 copy-start.4
  42.2 0.6 copy-start.5
  42.8 58.6 %copy-start.6 = (bf16[4096]{0:T(1024)(128)(2,1)S(1)}, bf16[4096]{0:T(1024)(128)(2,1)}, u32[]{:S(2)}) copy-start(bf16[4096]{0:T(1024)(128)(2,1)} %param.23) | copy-start | bytes 24580
